TPU v7x, 32 devices: a whole 2x2x4 slice. The times are simulated.
32 devices in a mesh: chol: 16 (over z, x, core), virt: 2 (over y).
Axes of the slice: x: 2, y: 2, z: 4, core: 2. Of those that a mesh axis runs over, the one named last changes fastest.
Arguments:
- amplitudes: bfloat16 [9600, 600], P('chol'), may hold values from -6 to 6
- chol_vectors: bfloat16 [128, 600, 600], P('chol', 'virt'), may hold values from -0.072753906 to 0.072753906
Outputs:
- sigma: float32 [9600, 600], P('chol', 'virt')
All inputs are finite; a program needn't handle non-finite values.
Results may differ from a plain program's by a relative error of at most 0.0042.
Values may be sent and summed in bfloat16 or wider, within the bound.
A program may use at most 192 MiB of HBM per device.

v0:
```python
import functools

import jax
import jax.numpy as jnp
from jax import lax
from jax.experimental import pallas as pl
from jax.experimental.pallas import tpu as pltpu
from jax.sharding import PartitionSpec as P

MESH = pl.DeviceIdType.MESH
KEPT = 4


def up(size, unit):
    return -(-size // unit) * unit


def plain(amplitudes, chol_vectors):
    vec_count, row_share, orbitals = chol_vectors.shape
    turned = jnp.transpose(chol_vectors, (1, 2, 0)).reshape(row_share, orbitals * vec_count)
    local_flat = chol_vectors.reshape(vec_count * row_share, orbitals)
    ladder_half = jnp.dot(
        lax.all_gather(amplitudes, "chol", axis=0, tiled=True),
        local_flat.T,
        preferred_element_type=jnp.float32,
    ).astype(jnp.bfloat16)
    combos = ladder_half.shape[0] // orbitals
    half_blocks = ladder_half.reshape(combos, orbitals * vec_count, row_share)
    sigma_terms = jnp.einsum(
        "ak,nkb->nab",
        lax.all_gather(turned, "virt", axis=0, tiled=True),
        half_blocks,
        preferred_element_type=jnp.float32,
    )
    sigma_terms = sigma_terms.reshape(combos * orbitals, row_share)
    return lax.psum_scatter(sigma_terms, "chol", scatter_dimension=0, tiled=True)


def kernel(ring, r_in, l_in, out, rbuf, lbuf, xbuf, xtmp, acc, sendbuf, recvbuf,
           loc_sem, r_send, r_recv, d_send, d_recv, y_send, y_recv, f_send, f_recv,
           p_send, p_recv):
    half = ring // 2
    chol, virt = lax.axis_index("chol"), lax.axis_index("virt")
    core, chip = chol % 2, chol // 2
    odd = chip % 2
    pos = (1 - odd) * (chip // 2) + odd * (ring - 1 - chip // 2)
    vecs, rows, width = l_in.shape
    tall = r_in.shape[0]

    def at(offset):
        there = (pos + offset + ring) % ring
        back = there // half
        q = (1 - back) * 2 * there + back * (2 * (ring - 1 - there) + 1)
        return (q * 2 + core, virt)

    partner, across = (chip * 2 + 1 - core, virt), (chol, 1 - virt)

    barrier = pltpu.get_barrier_semaphore()
    for peer in [at(r) for r in range(1, ring)] + [partner, across]:
        pl.semaphore_signal(barrier, inc=1, device_id=peer, device_id_type=MESH)

    cp_r = pltpu.make_async_copy(r_in, rbuf.at[0, pl.ds(0, tall)], loc_sem.at[0])
    cp_l = pltpu.make_async_copy(l_in, lbuf.at[virt, core], loc_sem.at[1])
    cp_r.start()
    cp_l.start()
    if width > tall:
        rbuf[:, tall:, :] = jnp.zeros((ring, width - tall, width), rbuf.dtype)
    cp_r.wait()
    cp_l.wait()
    pl.semaphore_wait(barrier, ring + 1)

    def remote(src, dst, s, r, to):
        return pltpu.make_async_remote_copy(
            src_ref=src, dst_ref=dst, send_sem=s, recv_sem=r, device_id=to, device_id_type=MESH)

    def hop_up(d):
        return remote(rbuf.at[d - 1, pl.ds(0, tall)], rbuf.at[d, pl.ds(0, tall)],
                      r_send.at[d], r_recv.at[d], at(1))

    def hop_down(d):
        src = 0 if d == ring - 1 else d + 1
        return remote(rbuf.at[src, pl.ds(0, tall)], rbuf.at[d, pl.ds(0, tall)],
                      r_send.at[d], r_recv.at[d], at(-1))

    hops = {d: hop_up(d) for d in range(1, half + 1)}
    hops.update({d: hop_down(d) for d in range(half + 1, ring)})
    give = remote(lbuf.at[virt, core], lbuf.at[virt, core], d_send, d_recv, partner)
    cross = [remote(lbuf.at[virt, core, j], lbuf.at[virt, core, j], y_send.at[j], y_recv.at[j], across)
             for j in range(vecs)]
    share = [remote(lbuf.at[1 - virt, core, j], lbuf.at[1 - virt, core, j], f_send.at[j], f_recv.at[j], partner)
             for j in range(vecs)]

    hops[1].start()
    hops[ring - 1].start()
    for c in cross:
        c.start()
    give.start()

    part = vecs // 2
    chunk = part * rows

    def stage_one(slot, c, j, dst, first):
        left = lbuf[virt, c, pl.ds(j * part, part)].reshape(chunk, width)
        dst[pl.ds(first, chunk), :] = lax.dot_general(
            left, rbuf[slot], (((1,), (1,)), ((), ())),
            preferred_element_type=jnp.float32).astype(jnp.bfloat16)

    def keep(slot, k):
        @pl.loop(0, 4)
        def _(i):
            stage_one(slot, i // 2, i % 2, xbuf.at[k], pl.multiple_of(i * chunk, chunk))

    give.wait_recv()
    keep(0, 0)
    kept = {0: 0}
    moved = 0
    for s in range(1, half + 1):
        due = [s] if s == half else [s, ring - s]
        for d in due:
            hops[d].wait_recv()
        if s < half:
            hops[s + 1].start()
            if ring - s - 1 > half:
                hops[ring - s - 1].start()
        goal = (vecs * s) // half
        for j in range(moved, goal):
            cross[j].wait_recv()
            share[j].start()
        moved = goal
        for d in due:
            if len(kept) < KEPT:
                kept[d] = len(kept)
                keep(d, kept[d])
    for j in range(vecs):
        share[j].wait_recv()

    def second(p, x0, x1):
        both = jnp.concatenate([x0, x1], axis=0)
        c, j = p // vecs, p % vecs
        weights = jnp.concatenate([lbuf[0, c, j], lbuf[1, c, j]], axis=0)
        acc[...] += lax.dot_general(both, weights, (((1,), (1,)), ((), ())),
                                    preferred_element_type=jnp.float32)

    far = sorted((d for d in range(ring) if d not in kept), key=lambda d: -min(d, ring - d))
    near = sorted(kept, key=lambda d: -min(d, ring - d))
    order = far + near
    posts = []
    for g in range(0, ring, 2):
        pair = order[g:g + 2]
        acc[...] = jnp.zeros_like(acc)
        if pair[0] in kept:
            @pl.loop(0, 2 * vecs)
            def _(p):
                first = pl.ds(pl.multiple_of(p * rows, rows), rows)
                second(p, xbuf[kept[pair[0]], first, :], xbuf[kept[pair[1]], first, :])
        else:
            @pl.loop(0, 4)
            def _(i):
                for t in range(2):
                    stage_one(pair[t], i // 2, i % 2, xtmp.at[t], 0)

                @pl.loop(0, part)
                def _(m):
                    first = pl.ds(pl.multiple_of(m * rows, rows), rows)
                    second(i * part + m, xtmp[0, first, :], xtmp[1, first, :])
        for t in range(2):
            d = pair[t]
            if d == 0:
                out[...] = acc[pl.ds(t * rows, rows), :]
            else:
                sendbuf[d - 1] = acc[pl.ds(t * rows, rows), :].astype(jnp.bfloat16)
                post = remote(sendbuf.at[d - 1], recvbuf.at[d - 1], p_send.at[d - 1], p_recv.at[d - 1], at(-d))
                post.start()
                posts.append((d, post))
    for d, post in posts:
        post.wait_recv()
        out[...] += recvbuf[d - 1].astype(jnp.float32)
    for d, post in posts:
        post.wait_send()
    for d in hops:
        hops[d].wait_send()
    for c in cross + share:
        c.wait_send()
    give.wait_send()


def fused(ring, amplitudes, chol_vectors):
    vecs, share, orbitals = chol_vectors.shape
    rows, width, tall = up(share, 16), up(orbitals, 128), up(orbitals, 16)
    bf, f32 = jnp.bfloat16, jnp.float32
    r = jnp.pad(amplitudes, ((0, tall - orbitals), (0, width - orbitals)))
    l = jnp.pad(chol_vectors, ((0, 0), (0, rows - share), (0, width - orbitals)))
    dma = pltpu.SemaphoreType.DMA
    turned = pl.pallas_call(
        functools.partial(kernel, ring),
        out_shape=jax.ShapeDtypeStruct((rows, 2 * rows), f32),
        in_specs=[pl.BlockSpec(memory_space=pl.ANY)] * 2,
        out_specs=pl.BlockSpec(memory_space=pltpu.VMEM),
        scratch_shapes=[
            pltpu.VMEM((ring, width, width), bf),
            pltpu.VMEM((2, 2, vecs, rows, width), bf),
            pltpu.VMEM((KEPT, 2 * vecs * rows, width), bf),
            pltpu.VMEM((2, vecs // 2 * rows, width), bf),
            pltpu.VMEM((2 * rows, 2 * rows), f32),
            pltpu.VMEM((ring - 1, rows, 2 * rows), bf),
            pltpu.VMEM((ring - 1, rows, 2 * rows), bf),
            dma((2,)), dma((ring,)), dma((ring,)), dma, dma,
            dma((vecs,)), dma((vecs,)), dma((vecs,)), dma((vecs,)),
            dma((ring - 1,)), dma((ring - 1,)),
        ],
        compiler_params=pltpu.CompilerParams(
            collective_id=0, has_side_effects=True, vmem_limit_bytes=67043328),
        name="ladder",
    )(r, l)
    sides = jnp.concatenate([turned[:share, :share], turned[:share, rows:rows + share]], axis=1)
    return sides.T


def solution(mesh):
    chol, virt = mesh.shape["chol"], mesh.shape["virt"]

    def shards(amplitudes, chol_vectors):
        vecs, share, orbitals = chol_vectors.shape
        fits = virt == 2 and chol % 4 == 0 and chol >= 16 and vecs % 2 == 0
        if fits and amplitudes.shape[0] == orbitals:
            return fused(chol // 2, amplitudes, chol_vectors)
        return plain(amplitudes, chol_vectors)

    placed = (P("chol", None), P("chol", "virt", None))
    return jax.shard_map(
        shards, mesh=mesh, in_specs=placed, out_specs=P("chol", "virt"), check_vma=False
    )
```

profile of v0, /device:TPU:1, one launch (start us, length us, event | category | flops | bytes accessed | tf_op | source)
XLA Modules:
  0.0 180.3 jit_solution(17695934033060782374)
XLA Ops:
  0.0 2.3 %copy.3 = bf16[8,300,600]{2,1,0:T(8,128)(2,1)S(1)} copy(bf16[8,300,600]{2,0,1:T(8,128)(2,1)} %param.3) | data formatting | bytes 5760000 | tf_op args[1]
  2.3 0.0 copy-start
  2.3 1.9 %pad.9.l_in = bf16[8,304,640]{2,1,0:T(8,128)(2,1)} pad(bf16[8,300,600]{2,1,0:T(8,128)(2,1)S(1)} %copy.3, bf16[]{:T(256)} %constant.2.clone.1), padding=0_0x0_4x0_40 | pad | bytes 5992962 | tf_op jit(solution)/shard_map/jit(_pad)/pad | solution.py:192
  4.2 0.0 copy-done
  4.2 0.9 pad.8.r_in
  5.2 172.7 %ladder.1 = f32[304,608]{1,0:T(8,128)} custom-call(bf16[608,640]{1,0:T(8,128)(2,1)} %pad.8.r_in, bf16[8,304,640]{2,1,0:T(8,128)(2,1)} %pad.9.l_in), custom_call_target="tpu_custom_call" | custom-call | tf_op jit(solution)/shard_map/ladder/pallas_call | solution.py:194
  177.9 1.3 fusion
  179.3 1.1 maximum_bitcast_fusion
Async XLA Ops:
  2.3 2.0 %copy-start = (bf16[600,600]{1,0:T(8,128)(2,1)S(1)}, bf16[600,600]{1,0:T(8,128)(2,1)}, u32[]{:S(2)}) copy-start(bf16[600,600]{1,0:T(8,128)(2,1)} %param.2) | copy-start | bytes 2160004
where the time goes:
time: 181 us; the launch traced here: 180 us
  Pallas kernels  173 us (96%)
  local copies, waits for them, and re-layouts  6.51 us (4%)
    pallas_call x1, Pallas kernels, fused(): pl.pallas_call(functools.partial(kernel, ring), out_shape=jax.ShapeDtypeS...  173 us

commit v1 on v0

v1 whole, which is shorter than its diff:
```python
import functools

import jax
import jax.numpy as jnp
from jax import lax
from jax.experimental import pallas as pl
from jax.experimental.pallas import tpu as pltpu
from jax.sharding import PartitionSpec as P

MESH = pl.DeviceIdType.MESH
NT = (((1,), (1,)), ((), ()))
NN = (((1,), (0,)), ((), ()))
VMEM_LIMIT = 67043328
SIDE = 256


def up(size, unit):
    return -(-size // unit) * unit


def plain(amplitudes, chol_vectors):
    vec_count, row_share, orbitals = chol_vectors.shape
    turned = jnp.transpose(chol_vectors, (1, 2, 0)).reshape(row_share, orbitals * vec_count)
    local_flat = chol_vectors.reshape(vec_count * row_share, orbitals)
    ladder_half = jnp.dot(
        lax.all_gather(amplitudes, "chol", axis=0, tiled=True),
        local_flat.T,
        preferred_element_type=jnp.float32,
    ).astype(jnp.bfloat16)
    combos = ladder_half.shape[0] // orbitals
    half_blocks = ladder_half.reshape(combos, orbitals * vec_count, row_share)
    sigma_terms = jnp.einsum(
        "ak,nkb->nab",
        lax.all_gather(turned, "virt", axis=0, tiled=True),
        half_blocks,
        preferred_element_type=jnp.float32,
    )
    sigma_terms = sigma_terms.reshape(combos * orbitals, row_share)
    return lax.psum_scatter(sigma_terms, "chol", scatter_dimension=0, tiled=True)


def kernel(ring, r_in, l_in, out, rbuf, lbuf, xa, xb,
           mine_a, give_a, got_a, rin_a,
           mine_s, give_s, got_s, rin_s,
           mine_t, give_t, got_t, rin_t, own_s, own_t, res,
           loc_sem, h_send, h_recv, g_send, g_recv, y_send, y_recv, z_send, z_recv,
           da_send, da_recv, ds_send, ds_recv, dt_send, dt_recv,
           ra_send, ra_recv, rs_send, rs_recv, rt_send, rt_recv, f_send, f_recv):
    half = ring // 2
    chol, virt = lax.axis_index("chol"), lax.axis_index("virt")
    core, chip = chol % 2, chol // 2
    odd = chip % 2
    pos = (1 - odd) * (chip // 2) + odd * (ring - 1 - chip // 2)
    vecs, rows, width = l_in.shape
    tall = 2 * rows
    cut = tall // SIDE * SIDE
    rest = tall - cut
    first_cross = cut - rows
    hc, hr = cut // 2, rest // 2
    lane = up(rest, 128)
    pad = width - tall
    same = 1 - (core + virt) % 2
    sgn = 2 * same - 1

    def at(offset):
        there = (pos + offset + ring) % ring
        back = there // half
        q = (1 - back) * 2 * there + back * (2 * (ring - 1 - there) + 1)
        return (q * 2 + core, virt)

    partner, across = (chip * 2 + 1 - core, virt), (chol, 1 - virt)
    keeper, taker = (chip * 2 + virt, virt), (chip * 2 + virt, 1 - virt)
    peers = [at(1), at(-1), partner, across, (chip * 2 + 1 - core, 1 - virt)]

    barrier = pltpu.get_barrier_semaphore()
    for peer in peers:
        pl.semaphore_signal(barrier, inc=1, device_id=peer, device_id_type=MESH)

    cp_r = pltpu.make_async_copy(r_in, rbuf.at[0], loc_sem.at[0])
    cp_l = pltpu.make_async_copy(l_in, lbuf.at[:, pl.ds(0, rows)], loc_sem.at[1])

    @pl.when(same == 1)
    def _():
        cp_r.start()

    cp_l.start()

    @pl.loop(0, ring - 1)
    def _(d):
        xa[d, pl.ds(vecs * tall, pad), :] = jnp.zeros((pad, cut), xa.dtype)

    xb[pl.ds(vecs * tall, pad), :] = jnp.zeros((pad, 2 * lane), xb.dtype)
    cp_l.wait()

    @pl.when(same == 1)
    def _():
        cp_r.wait()

    pl.semaphore_wait(barrier, len(peers))

    def remote(src, dst, s, r, to):
        return pltpu.make_async_remote_copy(
            src_ref=src, dst_ref=dst, send_sem=s, recv_sem=r, device_id=to, device_id_type=MESH)

    def mslot(s):
        return (s * sgn + ring) % ring

    def gslot(s):
        return (ring - s * sgn) % ring

    up_rows = pl.ds(pl.multiple_of((1 - same) * rows, rows), rows)
    other_rows = pl.ds(pl.multiple_of(same * rows, rows), rows)

    def hop(s):
        return remote(rbuf.at[mslot(s - 1)], rbuf.at[mslot(s)], h_send.at[s], h_recv.at[s], at(sgn))

    def half_hop():
        return remote(rbuf.at[mslot(half - 1), up_rows], rbuf.at[half, up_rows],
                      h_send.at[half], h_recv.at[half], at(sgn))

    def give(s):
        return remote(rbuf.at[mslot(s)], rbuf.at[mslot(s)], g_send.at[s], g_recv.at[s], partner)

    def taken(s):
        return remote(rbuf.at[gslot(s)], rbuf.at[gslot(s)], g_send.at[s], g_recv.at[s], partner)

    def half_give(where):
        return remote(rbuf.at[half, where], rbuf.at[half, where], g_send.at[half], g_recv.at[half], partner)

    def cross_a(p):
        return remote(lbuf.at[p, pl.ds(0, first_cross)], lbuf.at[p, pl.ds(rows, first_cross)],
                      y_send.at[p], y_recv.at[p], across)

    def cross_b(p):
        return remote(lbuf.at[p, pl.ds(first_cross, rest)], lbuf.at[p, pl.ds(cut, rest)],
                      z_send.at[p], z_recv.at[p], across)

    for p in range(vecs):
        cross_a(p).start()
    for p in range(vecs):
        cross_b(p).start()

    own = remote(rbuf.at[0], rbuf.at[0], g_send.at[0], g_recv.at[0], partner)

    @pl.when(same == 1)
    def _():
        own.start()

    @pl.when(same == 0)
    def _():
        own.wait_recv()

    hop(1).start()

    def held(d):
        return d - 1 + half * jnp.where(d == 0, 1, 0)

    def stage_one(d, p, count, lo, hi, to=None):
        size = hi - lo
        weights = lbuf[pl.ds(p, count), lo:hi, :].reshape(count * size, width)
        y = lax.dot_general(rbuf[d], weights, NT, preferred_element_type=jnp.float32).astype(jnp.bfloat16)
        for i in range(count):
            if to is None:
                xa[held(d), pl.ds((p + i) * tall, tall), lo:hi] = y[:, i * size:(i + 1) * size]
            else:
                to[pl.ds((p + i) * tall, tall), lo:hi] = y[:, i * size:(i + 1) * size]

    def arrived(p, count):
        for q in range(p, p + count):
            cross_a(q).wait_recv()

    pair = max(vecs // 4, 1)
    stage_one(0, 0, vecs, 0, SIDE, xb)

    @pl.loop(1, half + 2)
    def _(s):
        @pl.when(s < half)
        def _():
            hop(s).wait_recv()

            @pl.when(s + 1 < half)
            def _():
                hop(s + 1).start()

            @pl.when(s + 1 == half)
            def _():
                half_hop().start()

            give(s).start()

        @pl.when(s == half)
        def _():
            half_hop().wait_recv()
            half_give(up_rows).start()
            half_give(other_rows).wait_recv()

        per = jnp.where(s < half, 2, 1)

        @pl.loop(0, jnp.where(s > half, 0, per))
        def _(t):
            @pl.when(t == 1)
            def _():
                taken(s).wait_recv()

            stage_one(((1 - 2 * t) * s * sgn + 2 * ring) % ring, 0, vecs, 0, SIDE)

        batch = jnp.where(s > half, 2, s - 1)

        @pl.when((s < 3) | (s > half))
        def _():
            for q in range(pair):
                cross_a(batch * pair + q).wait_recv()

        groups = jnp.where(s == 1, 1, jnp.where(s == 2, 3, 2))

        @pl.loop(0, jnp.where(s > half, ring - 1, groups * per))
        def _(k):
            second = jnp.where(k < per, 0, 1)
            mirror = s + second * (1 - groups + k // per)
            d = jnp.where(s > half, k + 1, mirror + k % per * (ring - 2 * mirror))
            stage_one(d, jnp.where(s > half, 2, second) * pair, pair, SIDE, cut)

    arrived(3 * pair, vecs - 3 * pair)

    def flat(base, size):
        halves = []
        for c in (core, 1 - core):
            first = pl.ds(pl.multiple_of(base + c * size, 16), size)
            halves.append(jnp.concatenate([lbuf[p, first, :] for p in range(vecs)], axis=1))
        return jnp.concatenate(halves, axis=0)

    def deep(load):
        return jnp.concatenate([load(pl.ds(p * tall, width)) for p in range(vecs)], axis=0)

    def dot(left, right):
        return lax.dot_general(left, right, NN, preferred_element_type=jnp.float32)

    def slot_of(j, t):
        return (half + j) * (1 - t) + t * ((half - j) % half)

    def pass_on(d, j, t, src, rin, s, r):
        u = (1 - t) * jnp.where(j == 0, 1 - core, 1)
        raised = (d + 1) * (1 - (d + 1) // ring) + half * ((d + 1) // ring)
        to = u * raised + (1 - u) * (d - 1)
        return remote(src, rin.at[to], s.at[d], r.at[to], at(2 * u - 1))

    def has_input(j, t):
        given = jnp.where(t == 0, 1 - core, core)
        return jnp.where(j == 0, 0, jnp.where(j == 1, given, 1)) == 1

    def incoming(rin, s, r, d):
        return remote(rin.at[d], rin.at[d], s.at[d], r.at[d], at(1))

    def turn(i):
        if isinstance(i, int):
            return ((i + 1) // 2, (i + 1) % 2 if i else 0)
        return (i + 1) // 2, (i + 1) % 2 * jnp.where(i == 0, 0, 1)

    def a_slot(i):
        j, t = turn(i)
        return slot_of(j, t) % ring

    def hand_a(i):
        d = a_slot(i)
        return remote(give_a.at[i % 2], got_a.at[d], da_send.at[i % 2], da_recv.at[d], partner)

    def combine_a(i):
        j, t = turn(i)
        d = a_slot(i)
        hand_a(i).wait_recv()

        @pl.when(has_input(j, t))
        def _():
            incoming(rin_a, ra_send, ra_recv, d).wait_recv()
            mine_a[i % 2] += rin_a[d].astype(jnp.float32)

        got_a[d] = (mine_a[i % 2] + got_a[d].astype(jnp.float32)).astype(jnp.bfloat16)
        pass_on(d, j, t, got_a.at[d], rin_a, ra_send, ra_recv).start()

    def big(i, d):
        total = None
        for p in range(0, vecs, 2):
            left = jnp.concatenate([jnp.concatenate([lbuf[q, pl.ds(pl.multiple_of(c * hc, 16), hc), :]
                                                     for q in (p, p + 1)], axis=1) for c in (core, 1 - core)], axis=0)
            right = jnp.concatenate([xa[held(d), pl.ds(q * tall, width), :] for q in (p, p + 1)], axis=0)
            o = dot(left, right)
            total = o if total is None else total + o
        mine_a[i % 2] = total[:hc]
        give_a[i % 2] = total[hc:].astype(jnp.bfloat16)
        hand_a(i).start()

    def strip(j, t):
        o = dot(flat(cut, hr), deep(lambda k: xa[held(slot_of(j, t)), k, :]))
        mine_t[j % 2, t] = o[:hr]
        give_t[j % 2, t] = o[hr:].astype(jnp.bfloat16)

    @pl.loop(0, ring - 1)
    def _(i):
        d = a_slot(i)
        stage_one(d, 3 * pair, vecs - 3 * pair, SIDE, cut)

        @pl.when(i >= 2)
        def _():
            hand_a(i - 2).wait_send()

        big(i, d)

        @pl.when(i > 0)
        def _():
            combine_a(i - 1)

    for p in range(vecs):
        cross_b(p).wait_recv()

    final = ring - 1

    @pl.loop(0, 1)
    def _(t):
        strip(0, t)

    combine_a(final - 1)

    @pl.loop(0, vecs)
    def _(p):
        where = pl.ds(pl.multiple_of(p * tall, 16), tall)
        xa[half - 1, where, 0:SIDE] = xb[where, :]

    @pl.loop(0, 2)
    def _(k):
        stage_one(0, k * (vecs // 2), vecs // 2, SIDE, cut)

    hand_a(final - 2).wait_send()

    @pl.loop(final, final + 1)
    def _(i):
        big(i, a_slot(i))

    mine_rows_a = pl.ds(pl.multiple_of(core * hc, 16), hc)
    mine_rows_t = pl.ds(pl.multiple_of(cut + core * hr, 16), hr)
    mine_rows_s = pl.ds(pl.multiple_of(core * rows, 16), rows)
    keep_w = up(rows, 128)
    low = rows // 128 * 128

    far_a = remote(mine_a.at[final % 2, :, pl.ds(low, cut - low)], res.at[mine_rows_a, pl.ds(0, cut - low)],
                   f_send.at[0], f_recv.at[3 * core], taker)
    by_a = remote(mine_a.at[final % 2, :, pl.ds(0, keep_w)], res.at[mine_rows_a, pl.ds(0, keep_w)],
                  f_send.at[3], f_recv.at[0], keeper)

    def finish_a():
        hand_a(final).wait_recv()
        for d in (0, half):
            incoming(rin_a, ra_send, ra_recv, d).wait_recv()
        mine_a[final % 2] += (got_a[0].astype(jnp.float32) + rin_a[0].astype(jnp.float32)
                              + rin_a[half].astype(jnp.float32))
        far_a.start()

        @pl.when(same == 0)
        def _():
            by_a.start()

        @pl.when(same == 1)
        def _():
            res[mine_rows_a, 0:keep_w] = mine_a[final % 2, :, 0:keep_w]

    def hand_s(j):
        return remote(give_s.at[j % 2], got_s.at[j], ds_send.at[j % 2], ds_recv.at[j], partner)

    def hand_t(j):
        return remote(give_t.at[j % 2], got_t.at[j], dt_send.at[j % 2], dt_recv.at[j], partner)

    def combine_b(j, t):
        d = slot_of(j, t)
        cols = slice(t * lane, (t + 1) * lane)

        if t == 1:
            @pl.when(j == 0)
            def _():
                own_s[...] = mine_s[0, :, cols] + got_s[0, :, cols].astype(jnp.float32)
                own_t[...] = mine_t[0, t] + got_t[0, t].astype(jnp.float32)

        @pl.when(has_input(j, t))
        def _():
            incoming(rin_s, rs_send, rs_recv, d).wait_recv()
            incoming(rin_t, rt_send, rt_recv, d).wait_recv()
            mine_s[j % 2, :, cols] += rin_s[d].astype(jnp.float32)
            mine_t[j % 2, t] += rin_t[d].astype(jnp.float32)

        @pl.when(d != 0)
        def _():
            got_s[j, :, cols] = (mine_s[j % 2, :, cols] + got_s[j, :, cols].astype(jnp.float32)).astype(jnp.bfloat16)
            got_t[j, t] = (mine_t[j % 2, t] + got_t[j, t].astype(jnp.float32)).astype(jnp.bfloat16)
            pass_on(d, j, t, got_s.at[j, :, pl.ds(t * lane, lane)], rin_s, rs_send, rs_recv).start()
            pass_on(d, j, t, got_t.at[j, t], rin_t, rt_send, rt_recv).start()

    def handed(j):
        hand_s(j).wait_recv()
        hand_t(j).wait_recv()

    @pl.loop(0, half)
    def _(j):
        @pl.loop(0, 2)
        def _(t):
            d = slot_of(j, t)
            pieces = []
            for p in range(vecs):
                pieces.append(lbuf[p, cut:tall, :])
                if lane > rest:
                    pieces.append(jnp.zeros((lane - rest, width), lbuf.dtype))
            y = lax.dot_general(rbuf[d], jnp.concatenate(pieces, axis=0), NT,
                                preferred_element_type=jnp.float32).astype(jnp.bfloat16)
            for p in range(vecs):
                xb[pl.ds(p * tall, tall), pl.ds(pl.multiple_of(t * lane, lane), lane)] = y[:, p * lane:(p + 1) * lane]

        @pl.when(j >= 2)
        def _():
            hand_s(j - 2).wait_send()
            hand_t(j - 2).wait_send()

        @pl.loop(0, 2)
        def _(t):
            @pl.when(j + t > 0)
            def _():
                strip(j, t)

        hand_t(j).start()

        @pl.loop(0, 1)
        def _(t):
            o = dot(flat(0, rows), deep(lambda k: xb[k, :]))
            mine_s[j % 2] = o[:rows]
            give_s[j % 2] = o[rows:].astype(jnp.bfloat16)

        hand_s(j).start()

        @pl.when(j == 1)
        def _():
            finish_a()

        @pl.when(j > 0)
        def _():
            handed(j - 1)
            for t in range(2):
                combine_b(j - 1, t)

    end = half - 1
    handed(end)
    for t in range(2):
        combine_b(end, t)
    for d in (0, half):
        incoming(rin_s, rs_send, rs_recv, d).wait_recv()
        incoming(rin_t, rt_send, rt_recv, d).wait_recv()
    own_s[...] += rin_s[0].astype(jnp.float32) + rin_s[half].astype(jnp.float32)
    own_t[...] += rin_t[0].astype(jnp.float32) + rin_t[half].astype(jnp.float32)
    far_s = remote(own_s, res.at[mine_rows_s, pl.ds(cut - low, lane)],
                   f_send.at[2], f_recv.at[3 * core + 2], taker)
    far_t = remote(own_t.at[:, pl.ds(low, cut - low)], res.at[mine_rows_t, pl.ds(0, cut - low)],
                   f_send.at[1], f_recv.at[3 * core + 1], taker)
    by_t = remote(own_t.at[:, pl.ds(0, keep_w)], res.at[mine_rows_t, pl.ds(0, keep_w)],
                  f_send.at[4], f_recv.at[1], keeper)
    far_s.start()
    far_t.start()

    @pl.when(same == 0)
    def _():
        by_t.start()
        for c in range(2):
            rows_a = pl.ds(c * hc, hc)
            rows_t = pl.ds(cut + c * hr, hr)
            rows_s = pl.ds(c * rows, rows)
            ref = res.at[rows_a, pl.ds(0, cut - low)]
            remote(ref, ref, f_send.at[0], f_recv.at[3 * c], across).wait_recv()
            ref = res.at[rows_t, pl.ds(0, cut - low)]
            remote(ref, ref, f_send.at[1], f_recv.at[3 * c + 1], across).wait_recv()
            ref = res.at[rows_s, pl.ds(cut - low, lane)]
            remote(ref, ref, f_send.at[2], f_recv.at[3 * c + 2], across).wait_recv()
        by_a.wait_send()
        by_t.wait_send()

    @pl.when(same == 1)
    def _():
        res[mine_rows_t, 0:keep_w] = own_t[:, 0:keep_w]
        other_a = pl.ds(pl.multiple_of((1 - core) * hc, 16), hc)
        other_t = pl.ds(pl.multiple_of(cut + (1 - core) * hr, 16), hr)
        ref = res.at[other_a, pl.ds(0, keep_w)]
        remote(ref, ref, f_send.at[3], f_recv.at[0], partner).wait_recv()
        ref = res.at[other_t, pl.ds(0, keep_w)]
        remote(ref, ref, f_send.at[4], f_recv.at[1], partner).wait_recv()

    for c in range(2):
        dst = (core * (1 - c) + (1 - core) * c) * rows
        cp = pltpu.make_async_copy(res.at[pl.ds(c * rows, rows)],
                                   out.at[pl.ds(pl.multiple_of(dst, 16), rows)], loc_sem.at[c])
        cp.start()

    far_a.wait_send()
    far_s.wait_send()
    far_t.wait_send()
    for i in (ring - 2, ring - 1):
        hand_a(i).wait_send()
    for j in (half - 2, half - 1):
        hand_s(j).wait_send()
        hand_t(j).wait_send()
    for d in range(1, ring):
        remote(got_a.at[d], rin_a.at[d], ra_send.at[d], ra_recv.at[d], partner).wait_send()
        remote(rin_s.at[d], rin_s.at[d], rs_send.at[d], rs_recv.at[d], partner).wait_send()
        remote(rin_t.at[d], rin_t.at[d], rt_send.at[d], rt_recv.at[d], partner).wait_send()
    for s in range(1, half):
        hop(s).wait_send()
        give(s).wait_send()
    half_hop().wait_send()
    half_give(up_rows).wait_send()
    for p in range(vecs):
        cross_a(p).wait_send()
        cross_b(p).wait_send()

    @pl.when(same == 1)
    def _():
        own.wait_send()

    for c in range(2):
        dst = (core * (1 - c) + (1 - core) * c) * rows
        pltpu.make_async_copy(res.at[pl.ds(c * rows, rows)],
                              out.at[pl.ds(pl.multiple_of(dst, 16), rows)], loc_sem.at[c]).wait()


def scratch(ring, vecs, share, orbitals):
    rows, width = up(share, 16), up(orbitals, 128)
    tall, half = 2 * rows, ring // 2
    cut = tall // SIDE * SIDE
    rest = tall - cut
    lane = up(rest, 128)
    keep_w = max(up(rows, 128), cut - rows // 128 * 128 + lane)
    deep = vecs * tall + width - tall
    bf, f32 = jnp.bfloat16, jnp.float32
    return [
        ((ring, tall, width), bf), ((vecs, tall, width), bf),
        ((ring - 1, deep, cut), bf), ((deep, 2 * lane), bf),
        ((2, cut // 2, cut), f32), ((2, cut // 2, cut), bf), ((ring, cut // 2, cut), bf), ((ring, cut // 2, cut), bf),
        ((2, rows, 2 * lane), f32), ((2, rows, 2 * lane), bf), ((half, rows, 2 * lane), bf), ((ring, rows, lane), bf),
        ((2, 2, rest // 2, cut), f32), ((2, 2, rest // 2, cut), bf), ((half, 2, rest // 2, cut), bf),
        ((ring, rest // 2, cut), bf),
        ((rows, lane), f32), ((rest // 2, cut), f32), ((tall, keep_w), f32),
    ]


def fits(chol, virt, amplitudes, chol_vectors):
    vecs, share, orbitals = chol_vectors.shape
    if virt != 2 or chol % 4 or chol < 16 or vecs % 4:
        return False
    if amplitudes.shape[0] != orbitals or 2 * share != orbitals:
        return False
    rows = up(share, 16)
    cut = 2 * rows // SIDE * SIDE
    if cut != 2 * SIDE or 2 * up(2 * rows - cut, 128) != SIDE or rows < SIDE or cut <= rows or (2 * rows - cut) % 32 or up(orbitals, 128) <= 2 * rows:
        return False
    used = 0
    for shape, kind in scratch(chol // 2, vecs, share, orbitals):
        size = jnp.dtype(kind).itemsize
        for n in shape:
            size *= n
        used += size
    return used < VMEM_LIMIT


def fused(ring, amplitudes, chol_vectors):
    vecs, share, orbitals = chol_vectors.shape
    rows, width = up(share, 16), up(orbitals, 128)
    tall, half = 2 * rows, ring // 2
    r = jnp.pad(amplitudes, ((0, tall - orbitals), (0, width - orbitals)))
    l = jnp.pad(chol_vectors, ((0, 0), (0, rows - share), (0, width - orbitals)))
    dma = pltpu.SemaphoreType.DMA
    bufs = [pltpu.VMEM(shape, kind) for shape, kind in scratch(ring, vecs, share, orbitals)]
    shape = scratch(ring, vecs, share, orbitals)[-1][0]
    turned = pl.pallas_call(
        functools.partial(kernel, ring),
        out_shape=jax.ShapeDtypeStruct(shape, jnp.float32),
        in_specs=[pl.BlockSpec(memory_space=pl.ANY)] * 2,
        out_specs=pl.BlockSpec(memory_space=pl.ANY),
        scratch_shapes=bufs + [
            dma((2,)), dma((half + 1,)), dma((half + 1,)), dma((half + 1,)), dma((half + 1,)),
            dma((vecs,)), dma((vecs,)), dma((vecs,)), dma((vecs,)),
            dma((2,)), dma((ring,)), dma((2,)), dma((half,)), dma((2,)), dma((half,)),
            dma((ring,)), dma((ring,)), dma((ring,)), dma((ring,)), dma((ring,)), dma((ring,)),
            dma((5,)), dma((6,)),
        ],
        compiler_params=pltpu.CompilerParams(
            collective_id=0, has_side_effects=True, vmem_limit_bytes=VMEM_LIMIT),
        name="ladder",
    )(r, l)
    skip = rows % 128
    here = lax.axis_index("chol") % 2 == lax.axis_index("virt")
    sides = jnp.where(here, turned[:, :share], turned[:, skip:skip + share])
    return jnp.concatenate([sides[:share], sides[rows:rows + share]], axis=0)


def solution(mesh):
    chol, virt = mesh.shape["chol"], mesh.shape["virt"]

    def shards(amplitudes, chol_vectors):
        if fits(chol, virt, amplitudes, chol_vectors):
            return fused(chol // 2, amplitudes, chol_vectors)
        return plain(amplitudes, chol_vectors)

    placed = (P("chol", None), P("chol", "virt", None))
    return jax.shard_map(
        shards, mesh=mesh, in_specs=placed, out_specs=P("chol", "virt"), check_vma=False
    )
```

time: 181 us -> 140 us (0.77)
  Pallas kernels: 173 us -> 132 us
    pallas_call x1, Pallas kernels: 173 us -> 132 us  [fused(): pl.pallas_call(functools.partial(kernel, ring), out_shape=jax.ShapeDtypeS...]
where the time goes in v1:
time: 140 us
  Pallas kernels  132 us (94%)
  local copies, waits for them, and re-layouts  6.41 us (5%)
  other arithmetic  1.85 us (1%)
    pallas_call x1, Pallas kernels, fused(): pl.pallas_call(functools.partial(kernel, ring), out_shape=jax.ShapeDtypeS...  132 us

profile of v1, /device:TPU:1, one launch (start us, length us, event | category | flops | bytes accessed | tf_op | source)
XLA Modules:
  0.0 139.9 jit_solution(16575065431981152938)
XLA Ops:
  0.0 2.3 %copy.3 = bf16[8,300,600]{2,1,0:T(8,128)(2,1)S(1)} copy(bf16[8,300,600]{2,0,1:T(8,128)(2,1)} %param.3) | data formatting | bytes 5760000 | tf_op args[1]
  2.3 0.0 copy-start
  2.3 1.9 %pad.9.l_in = bf16[8,304,640]{2,1,0:T(8,128)(2,1)} pad(bf16[8,300,600]{2,1,0:T(8,128)(2,1)S(1)} %copy.3, bf16[]{:T(256)} %constant.23.clone.1), padding=0_0x0_4x0_40 | pad | bytes 5992962 | tf_op jit(solution)/shard_map/jit(_pad)/pad | solution.py:570
  4.2 0.0 copy-done
  4.2 0.9 pad.8.r_in
  5.2 131.6 %ladder.1 = f32[608,384]{1,0:T(8,128)} custom-call(bf16[608,640]{1,0:T(8,128)(2,1)} %pad.8.r_in, bf16[8,304,640]{2,1,0:T(8,128)(2,1)} %pad.9.l_in), custom_call_target="tpu_custom_call" | custom-call | tf_op jit(solution)/shard_map/ladder/pallas_call | solution.py:574
  136.8 1.8 %slice_select_fusion = f32[608,300]{1,0:T(8,128)S(1)} fusion(f32[608,384]{1,0:T(8,128)} %ladder.1, pred[]{:T(512)S(6)} %eq.5), kind=kLoop, calls=%fused_computation | loop fusion | flops 182400 | bytes 2188801 | tf_op jit(solution)/shard_map/jit(_where)/select_n | solution.py:592
  138.6 0.1 fusion
  138.7 0.1 pad_maximum_fusion
  138.7 1.2 copy.4
Async XLA Ops:
  2.3 2.0 %copy-start = (bf16[600,600]{1,0:T(8,128)(2,1)S(1)}, bf16[600,600]{1,0:T(8,128)(2,1)}, u32[]{:S(2)}) copy-start(bf16[600,600]{1,0:T(8,128)(2,1)} %param.2) | copy-start | bytes 2160004

commit v2 on v1

--- a/solution.py
+++ b/solution.py
@@ -42,7 +42,7 @@
 def kernel(ring, r_in, l_in, out, rbuf, lbuf, xa, xb,
            mine_a, give_a, got_a, rin_a,
            mine_s, give_s, got_s, rin_s,
-           mine_t, give_t, got_t, rin_t, own_s, own_t, res,
+           mine_t, give_t, got_t, rin_t, own_s, own_t, out_s, out_t, in_s, in_t, res,
            loc_sem, h_send, h_recv, g_send, g_recv, y_send, y_recv, z_send, z_recv,
            da_send, da_recv, ds_send, ds_recv, dt_send, dt_recv,
            ra_send, ra_recv, rs_send, rs_recv, rt_send, rt_recv, f_send, f_recv):
@@ -108,24 +108,20 @@
     def gslot(s):
         return (ring - s * sgn) % ring
 
-    up_rows = pl.ds(pl.multiple_of((1 - same) * rows, rows), rows)
-    other_rows = pl.ds(pl.multiple_of(same * rows, rows), rows)
-
-    def hop(s):
-        return remote(rbuf.at[mslot(s - 1)], rbuf.at[mslot(s)], h_send.at[s], h_recv.at[s], at(sgn))
-
-    def half_hop():
-        return remote(rbuf.at[mslot(half - 1), up_rows], rbuf.at[half, up_rows],
-                      h_send.at[half], h_recv.at[half], at(sgn))
-
-    def give(s):
-        return remote(rbuf.at[mslot(s)], rbuf.at[mslot(s)], g_send.at[s], g_recv.at[s], partner)
-
-    def taken(s):
-        return remote(rbuf.at[gslot(s)], rbuf.at[gslot(s)], g_send.at[s], g_recv.at[s], partner)
-
-    def half_give(where):
-        return remote(rbuf.at[half, where], rbuf.at[half, where], g_send.at[half], g_recv.at[half], partner)
+    def rows_of(u):
+        return pl.ds(pl.multiple_of(u * rows, 16), rows)
+
+    def hop(s, u):
+        return remote(rbuf.at[mslot(s - 1), rows_of(u)], rbuf.at[mslot(s), rows_of(u)],
+                      h_send.at[2 * s + u], h_recv.at[2 * s + u], at(sgn))
+
+    def give(s, u):
+        ref = rbuf.at[mslot(s), rows_of(u)]
+        return remote(ref, ref, g_send.at[2 * s + u], g_recv.at[2 * s + u], partner)
+
+    def taken(s, u):
+        ref = rbuf.at[gslot(s), rows_of(u)]
+        return remote(ref, ref, g_send.at[2 * s + u], g_recv.at[2 * s + u], partner)
 
     def cross_a(p):
         return remote(lbuf.at[p, pl.ds(0, first_cross)], lbuf.at[p, pl.ds(rows, first_cross)],
@@ -140,17 +136,17 @@
     for p in range(vecs):
         cross_b(p).start()
 
-    own = remote(rbuf.at[0], rbuf.at[0], g_send.at[0], g_recv.at[0], partner)
-
     @pl.when(same == 1)
     def _():
-        own.start()
+        for u in range(2):
+            give(0, u).start()
+            hop(1, u).start()
 
     @pl.when(same == 0)
     def _():
-        own.wait_recv()
-
-    hop(1).start()
+        for u in range(2):
+            taken(0, u).wait_recv()
+            hop(1, u).start()
 
     def held(d):
         return d - 1 + half * jnp.where(d == 0, 1, 0)
@@ -165,6 +161,14 @@
             else:
                 to[pl.ds((p + i) * tall, tall), lo:hi] = y[:, i * size:(i + 1) * size]
 
+    def stage_rows(d, u):
+        weights = lbuf[:, 0:SIDE, :].reshape(vecs * SIDE, width)
+        y = lax.dot_general(rbuf[d, rows_of(u), :], weights, NT,
+                            preferred_element_type=jnp.float32).astype(jnp.bfloat16)
+        for p in range(vecs):
+            where = pl.ds(pl.multiple_of(p * tall + u * rows, 16), rows)
+            xa[held(d), where, 0:SIDE] = y[:, p * SIDE:(p + 1) * SIDE]
+
     def arrived(p, count):
         for q in range(p, p + count):
             cross_a(q).wait_recv()
@@ -174,35 +178,29 @@
 
     @pl.loop(1, half + 2)
     def _(s):
-        @pl.when(s < half)
-        def _():
-            hop(s).wait_recv()
-
-            @pl.when(s + 1 < half)
+        per = jnp.where(s < half, 2, 1)
+
+        @pl.loop(0, jnp.where(s > half, 0, 2 * per))
+        def _(k):
+            t = k % 2
+            alone = t * same + (1 - t) * (1 - same)
+            u = jnp.where(s < half, k // 2, alone)
+
+            @pl.when(t == 0)
             def _():
-                hop(s + 1).start()
-
-            @pl.when(s + 1 == half)
-            def _():
-                half_hop().start()
-
-            give(s).start()
-
-        @pl.when(s == half)
-        def _():
-            half_hop().wait_recv()
-            half_give(up_rows).start()
-            half_give(other_rows).wait_recv()
-
-        per = jnp.where(s < half, 2, 1)
-
-        @pl.loop(0, jnp.where(s > half, 0, per))
-        def _(t):
+                hop(s, u).wait_recv()
+
+                @pl.when((s + 1 < half) | ((s + 1 == half) & (u == 1 - same)))
+                def _():
+                    hop(s + 1, u).start()
+
+                give(s, u).start()
+
             @pl.when(t == 1)
             def _():
-                taken(s).wait_recv()
-
-            stage_one(((1 - 2 * t) * s * sgn + 2 * ring) % ring, 0, vecs, 0, SIDE)
+                taken(s, u).wait_recv()
+
+            stage_rows(((1 - 2 * t) * s * sgn + 2 * ring) % ring, u)
 
         batch = jnp.where(s > half, 2, s - 1)
 
@@ -451,9 +449,11 @@
         incoming(rin_t, rt_send, rt_recv, d).wait_recv()
     own_s[...] += rin_s[0].astype(jnp.float32) + rin_s[half].astype(jnp.float32)
     own_t[...] += rin_t[0].astype(jnp.float32) + rin_t[half].astype(jnp.float32)
-    far_s = remote(own_s, res.at[mine_rows_s, pl.ds(cut - low, lane)],
+    out_s[...] = own_s[...].astype(jnp.bfloat16)
+    out_t[...] = own_t[:, low:cut].astype(jnp.bfloat16)
+    far_s = remote(out_s, in_s.at[mine_rows_s],
                    f_send.at[2], f_recv.at[3 * core + 2], taker)
-    far_t = remote(own_t.at[:, pl.ds(low, cut - low)], res.at[mine_rows_t, pl.ds(0, cut - low)],
+    far_t = remote(out_t, in_t.at[pl.ds(pl.multiple_of(core * hr, 16), hr)],
                    f_send.at[1], f_recv.at[3 * core + 1], taker)
     by_t = remote(own_t.at[:, pl.ds(0, keep_w)], res.at[mine_rows_t, pl.ds(0, keep_w)],
                   f_send.at[4], f_recv.at[1], keeper)
@@ -465,14 +465,16 @@
         by_t.start()
         for c in range(2):
             rows_a = pl.ds(c * hc, hc)
-            rows_t = pl.ds(cut + c * hr, hr)
+            rows_t = pl.ds(c * hr, hr)
             rows_s = pl.ds(c * rows, rows)
             ref = res.at[rows_a, pl.ds(0, cut - low)]
             remote(ref, ref, f_send.at[0], f_recv.at[3 * c], across).wait_recv()
-            ref = res.at[rows_t, pl.ds(0, cut - low)]
+            ref = in_t.at[rows_t]
             remote(ref, ref, f_send.at[1], f_recv.at[3 * c + 1], across).wait_recv()
-            ref = res.at[rows_s, pl.ds(cut - low, lane)]
+            ref = in_s.at[rows_s]
             remote(ref, ref, f_send.at[2], f_recv.at[3 * c + 2], across).wait_recv()
+        res[0:tall, cut - low:cut - low + lane] = in_s[...].astype(jnp.float32)
+        res[cut:tall, 0:cut - low] = in_t[...].astype(jnp.float32)
         by_a.wait_send()
         by_t.wait_send()
 
@@ -504,18 +506,20 @@
         remote(got_a.at[d], rin_a.at[d], ra_send.at[d], ra_recv.at[d], partner).wait_send()
         remote(rin_s.at[d], rin_s.at[d], rs_send.at[d], rs_recv.at[d], partner).wait_send()
         remote(rin_t.at[d], rin_t.at[d], rt_send.at[d], rt_recv.at[d], partner).wait_send()
-    for s in range(1, half):
-        hop(s).wait_send()
-        give(s).wait_send()
-    half_hop().wait_send()
-    half_give(up_rows).wait_send()
+    for u in range(2):
+        for s in range(1, half):
+            hop(s, u).wait_send()
+            give(s, u).wait_send()
+    hop(half, 1 - same).wait_send()
+    give(half, 1 - same).wait_send()
     for p in range(vecs):
         cross_a(p).wait_send()
         cross_b(p).wait_send()
 
     @pl.when(same == 1)
     def _():
-        own.wait_send()
+        for u in range(2):
+            give(0, u).wait_send()
 
     for c in range(2):
         dst = (core * (1 - c) + (1 - core) * c) * rows
@@ -539,7 +543,8 @@
         ((2, rows, 2 * lane), f32), ((2, rows, 2 * lane), bf), ((half, rows, 2 * lane), bf), ((ring, rows, lane), bf),
         ((2, 2, rest // 2, cut), f32), ((2, 2, rest // 2, cut), bf), ((half, 2, rest // 2, cut), bf),
         ((ring, rest // 2, cut), bf),
-        ((rows, lane), f32), ((rest // 2, cut), f32), ((tall, keep_w), f32),
+        ((rows, lane), f32), ((rest // 2, cut), f32), ((rows, lane), bf), ((rest // 2, cut - rows // 128 * 128), bf),
+        ((tall, lane), bf), ((rest, cut - rows // 128 * 128), bf), ((tall, keep_w), f32),
     ]
 
 
@@ -577,7 +582,7 @@
         in_specs=[pl.BlockSpec(memory_space=pl.ANY)] * 2,
         out_specs=pl.BlockSpec(memory_space=pl.ANY),
         scratch_shapes=bufs + [
-            dma((2,)), dma((half + 1,)), dma((half + 1,)), dma((half + 1,)), dma((half + 1,)),
+            dma((2,)), dma((2 * half + 2,)), dma((2 * half + 2,)), dma((2 * half + 2,)), dma((2 * half + 2,)),
             dma((vecs,)), dma((vecs,)), dma((vecs,)), dma((vecs,)),
             dma((2,)), dma((ring,)), dma((2,)), dma((half,)), dma((2,)), dma((half,)),
             dma((ring,)), dma((ring,)), dma((ring,)), dma((ring,)), dma((ring,)), dma((ring,)),

time: 140 us -> 135 us (0.964)
  Pallas kernels: 132 us -> 126 us
    pallas_call x1, Pallas kernels: 132 us -> 126 us  [fused(): pl.pallas_call(functools.partial(kernel, ring), out_shape=jax.ShapeDtypeS...]
where the time goes in v2:
time: 135 us
  Pallas kernels  126 us (93%)
  local copies, waits for them, and re-layouts  6.41 us (5%)
  other arithmetic  1.85 us (1%)
    pallas_call x1, Pallas kernels, fused(): pl.pallas_call(functools.partial(kernel, ring), out_shape=jax.ShapeDtypeS...  126 us

profile of v2, /device:TPU:1, one launch (start us, length us, event | category | flops | bytes accessed | tf_op | source)
XLA Modules:
  0.0 134.7 jit_solution(11379274330447791228)
XLA Ops:
  0.0 2.3 %copy.3 = bf16[8,300,600]{2,1,0:T(8,128)(2,1)S(1)} copy(bf16[8,300,600]{2,0,1:T(8,128)(2,1)} %param.3) | data formatting | bytes 5760000 | tf_op args[1]
  2.3 0.0 copy-start
  2.3 1.9 %pad.9.l_in = bf16[8,304,640]{2,1,0:T(8,128)(2,1)} pad(bf16[8,300,600]{2,1,0:T(8,128)(2,1)S(1)} %copy.3, bf16[]{:T(256)} %constant.23.clone.1), padding=0_0x0_4x0_40 | pad | bytes 5992962 | tf_op jit(solution)/shard_map/jit(_pad)/pad | solution.py:575
  4.2 0.0 copy-done
  4.2 0.9 pad.8.r_in
  5.2 126.4 %ladder.1 = f32[608,384]{1,0:T(8,128)} custom-call(bf16[608,640]{1,0:T(8,128)(2,1)} %pad.8.r_in, bf16[8,304,640]{2,1,0:T(8,128)(2,1)} %pad.9.l_in), custom_call_target="tpu_custom_call" | custom-call | tf_op jit(solution)/shard_map/ladder/pallas_call | solution.py:579
  131.6 1.8 %slice_select_fusion = f32[608,300]{1,0:T(8,128)S(1)} fusion(f32[608,384]{1,0:T(8,128)} %ladder.1, pred[]{:T(512)S(6)} %eq.5), kind=kLoop, calls=%fused_computation | loop fusion | flops 182400 | bytes 2188801 | tf_op jit(solution)/shard_map/jit(_where)/select_n | solution.py:597
  133.4 0.1 fusion
  133.4 0.1 pad_maximum_fusion
  133.5 1.2 copy.4
Async XLA Ops:
  2.3 2.0 %copy-start = (bf16[600,600]{1,0:T(8,128)(2,1)S(1)}, bf16[600,600]{1,0:T(8,128)(2,1)}, u32[]{:S(2)}) copy-start(bf16[600,600]{1,0:T(8,128)(2,1)} %param.2) | copy-start | bytes 2160004
